TPU v7x, 128 devices: a whole 4x4x4 slice. The times are simulated.
128 devices in a mesh: row: 8 (over x, z_hi), col: 4 (over z_lo, core), depth: 4 (over y).
Axes of the slice: x: 4, y: 4, z: 4 (z_hi: 2, z_lo: 2; z = z_hi * 2 + z_lo), core: 2. Of those that a mesh axis runs over, the one named last changes fastest.
Arguments:
- acts: bfloat16 [8192, 5120], P(('depth', 'col'), 'row'), may hold values from -6 to 6
- grad_out: bfloat16 [8192, 13824], P(('depth', 'row'), 'col'), may hold values from -6 to 6
- weight: bfloat16 [5120, 13824], P('row', 'col'), may hold values from -0.078125 to 0.078125
- master: float32 [5120, 13824], P(('row', 'depth'), 'col'), may hold values from -0.078125 to 0.078125
- moment_one: float32 [5120, 13824], P(('row', 'depth'), 'col'), may hold values from -4 to 4
- moment_two: float32 [5120, 13824], P(('row', 'depth'), 'col'), may hold values from 0.05 to 2
Outputs:
- grad_in: bfloat16 [8192, 5120], P(('depth', 'col'), 'row')
- new_weight: bfloat16 [5120, 13824], P('row', 'col')
- new_master: float32 [5120, 13824], P(('row', 'depth'), 'col')
- new_moment_one: float32 [5120, 13824], P(('row', 'depth'), 'col')
- new_moment_two: float32 [5120, 13824], P(('row', 'depth'), 'col')
All inputs are finite; a program needn't handle non-finite values.
Results may differ from a plain program's by a relative error of at most 0.0035.
Values may be sent and summed in bfloat16 or wider, within the bound.
A program may use at most 128 MiB of HBM per device.

v0:
```python
import math
import jax
import jax.numpy as jnp
from jax import lax
from jax.sharding import PartitionSpec as P

STEP = 10


def in_order(parts, dim):
    dims = list(parts.shape[1:])
    dims[dim] *= parts.shape[0]
    return jnp.moveaxis(parts, 0, dim).reshape(dims)


def from_everyone(array, axis):
    count = lax.axis_size(axis)
    return lax.all_to_all(
        jnp.broadcast_to(array[None], (count, *array.shape)), axis, 0, 0, tiled=True
    )


def gathered_copies(array, axis, dim):
    return in_order(from_everyone(array, axis), dim)


def cut_along(array, dim, count):
    before, after = (array.shape[:dim], array.shape[dim + 1 :])
    return jnp.moveaxis(array.reshape(*before, count, -1, *after), dim, 0)


def sum_at_owner(array, axis, dim):
    parts = cut_along(array, dim, lax.axis_size(axis))
    arrived = lax.all_to_all(parts, axis, split_axis=0, concat_axis=0, tiled=True)
    return arrived.sum(axis=0)


def per_device(acts, grad_out, weight, master, moment_one, moment_two):
    whole_acts = gathered_copies(acts, "col", 0)
    tokens_total = acts.shape[0] * lax.axis_size("col") * lax.axis_size("depth")
    whole_cotangent = lax.all_gather(grad_out, "row", axis=0, tiled=True)
    picked = whole_cotangent
    input_sum = sum_at_owner(
        lax.dot_general(
            picked, weight, (((1,), (1,)), ((), ())), preferred_element_type=jnp.float32
        ),
        "col",
        0,
    )
    picked = whole_acts
    grad_sum = lax.psum_scatter(
        lax.dot_general(
            picked, whole_cotangent, (((0,), (0,)), ((), ())), preferred_element_type=jnp.float32
        ).astype(jnp.bfloat16),
        "depth",
        scatter_dimension=0,
        tiled=True,
    ).astype(jnp.float32)
    grad_in = input_sum.astype(jnp.bfloat16)
    grad = grad_sum * jnp.float32(1.0 / math.sqrt(tokens_total))
    new_moment_one = 0.9 * moment_one + 0.1 * grad
    new_moment_two = 0.95 * moment_two + 0.05 * grad * grad
    first_fix = 1.0 - 0.9**STEP
    second_fix = 1.0 - 0.95**STEP
    update = new_moment_one / first_fix / (jnp.sqrt(new_moment_two / second_fix) + 1e-08)
    new_master = master - 0.01 * (update + 0.1 * master)
    new_weight = lax.all_gather(new_master.astype(jnp.bfloat16), "depth", axis=0, tiled=True)
    return (grad_in, new_weight, new_master, new_moment_one, new_moment_two)


def solution(mesh):
    placed = (
        P(("depth", "col"), "row"),
        P(("depth", "row"), "col"),
        P("row", "col"),
        P(("row", "depth"), "col"),
        P(("row", "depth"), "col"),
        P(("row", "depth"), "col"),
    )
    return jax.shard_map(
        per_device,
        mesh=mesh,
        in_specs=placed,
        out_specs=(
            P(("depth", "col"), "row"),
            P("row", "col"),
            P(("row", "depth"), "col"),
            P(("row", "depth"), "col"),
            P(("row", "depth"), "col"),
        ),
        check_vma=False,
    )
```

profile of v0, /device:TPU:1, one launch (start us, length us, event | category | flops | bytes accessed | tf_op | source)
XLA Modules:
  0.0 352.9 jit_solution(4790569811612537850)
XLA Ops:
  7.2 0.0 copy-start.1
  7.2 0.0 all-gather.3.cloned.1.call-start
  7.2 0.7 all-gather.3.cloned.1.call-update
  7.9 0.0 reduce-scatter.2.cloned.1.call-start
  8.0 0.3 copy-done.1
  8.3 0.2 broadcast_in_dim.2
  8.5 50.5 %all_to_all.10 = bf16[4,512,640]{2,1,0:T(8,128)(2,1)S(1)} all-to-all(bf16[4,512,640]{2,1,0:T(8,128)(2,1)S(1)} %broadcast_in_dim.2), channel_id=1, replica_groups=mesh['row'=8,'col'=4,'depth'=4] {'col'}, dimensions={0} | all-to-all | bytes 5242880 | tf_op jit(solution)/shard_map/all_to_all | solution.py:18
  59.0 131.6 %all-gather.3.cloned.1.call-done = bf16[2048,3456]{1,0:T(8,128)(2,1)} async-done(((bf16[256,3456]{1,0:T(8,128)(2,1)}), bf16[2048,3456]{1,0:T(8,128)(2,1)}) %all-gather.3.cloned.1.call-update) | async-done | bytes 14155792 | tf_op jit(solution)/shard_map/all_gather | solution.py:41
  190.6 14.4 %convolution_convert_fusion = bf16[640,3456]{1,0:T(8,128)(2,1)} fusion(bf16[2048,640]{1,0:T(8,128)(2,1)S(1)} %bitcast.7, bf16[2048,3456]{1,0:T(8,128)(2,1)} %all-gather.3.cloned.1.call-done), kind=kOutput, calls=%fused_computation | convolution fusion | flops 9061908480 | bytes 21200896 | tf_op jit(solution)/shard_map/dot_general | solution.py:52
  205.1 0.0 copy-start
  205.1 0.0 reduce-scatter.2.cloned.1.call-update
  205.1 0.0 all-gather.5.cloned.1.call-start
  205.1 47.2 %reduce-scatter.2.cloned.1.call-done = bf16[160,3456]{1,0:T(8,128)(2,1)} async-done(((bf16[640,3456]{1,0:T(8,128)(2,1)}), bf16[160,3456]{1,0:T(8,128)(2,1)}) %reduce-scatter.2.cloned.1.call-update) | async-done | bytes 1105936 | tf_op jit(solution)/shard_map/reduce_scatter | solution.py:51
  252.3 0.0 copy-done
  252.3 7.0 %fusion.3 = (bf16[160,3456]{1,0:T(8,128)(2,1)}, f32[160,3456]{1,0:T(8,128)}, f32[160,3456]{1,0:T(8,128)}, f32[160,3456]{1,0:T(8,128)}) fusion(f32[160,3456]{1,0:T(8,128)S(1)} %copy-done, bf16[160,3456]{1,0:T(8,128)(2,1)} %reduce-scatter.2.cloned.1.call-done, f32[160,3456]{1,0:T(8,128)} %param.10, f32[160,3456]{1,0:T(8,128)} %param.11), kind=kLoop, calls=%fused_computation.8 | loop fusion | flops 9953280 | bytes 15482880 | tf_op jit(solution)/shard_map/convert_element_type | solution.py:67
  259.4 0.0 all-gather.5.cloned.1.call-update
  259.4 15.9 %fusion.6 = f32[2048,640]{1,0:T(8,128)S(1)} fusion(bf16[2048,3456]{1,0:T(8,128)(2,1)} %all-gather.3.cloned.1.call-done, bf16[640,3456]{1,0:T(8,128)(2,1)} %param.8), kind=kOutput, calls=%fused_computation.9 | convolution fusion | flops 9059696640 | bytes 23822336 | tf_op jit(solution)/shard_map/dot_general | solution.py:44
  275.3 62.6 %all_to_all.11 = f32[4,512,640]{2,1,0:T(8,128)} all-to-all(f32[4,512,640]{2,1,0:T(8,128)S(1)} %bitcast.6), channel_id=1, replica_groups=mesh['row'=8,'col'=4,'depth'=4] {'col'}, dimensions={0} | all-to-all | bytes 10485760 | tf_op jit(solution)/shard_map/all_to_all | solution.py:34
  337.9 3.8 %reduce_sum.9 = bf16[512,640]{1,0:T(8,128)(2,1)} reduce(f32[4,512,640]{2,1,0:T(8,128)} %all_to_all.11, f32[]{:T(128)} %constant.4.clone.1), dimensions={0}, to_apply=%region_0.0 | reduce | flops 983040 | bytes 5898244 | tf_op jit(solution)/shard_map/reduce_sum | solution.py:35
  341.7 0.0 all-gather.5.cloned.1.call-done
  341.7 4.6 %copy.12 = bf16[640,3456]{1,0:T(8,128)(2,1)} copy(bf16[640,3456]{1,0:T(8,128)(2,1)} %all-gather.5.cloned.1.call-done) | data formatting | bytes 8847360
Async XLA Ops:
  7.2 1.1 copy-start.1
  7.2 183.5 %all-gather.3.cloned.1.call-start = ((), (), s32[]{:S(2)}) async-start(), calls=%async_computation.3 | async-start | bytes 15925248 | tf_op jit(solution)/shard_map/all_gather | solution.py:41
  7.9 244.4 %reduce-scatter.2.cloned.1.call-start = ((), (), s32[]{:S(2)}) async-start(), calls=%async_computation.4 | async-start | bytes 5529600 | tf_op jit(solution)/shard_map/reduce_scatter | solution.py:51
  205.1 47.3 %copy-start = (f32[160,3456]{1,0:T(8,128)S(1)}, f32[160,3456]{1,0:T(8,128)}, u32[]{:S(2)}) copy-start(f32[160,3456]{1,0:T(8,128)} %param.9) | copy-start | bytes 6635524
  205.1 136.6 %all-gather.5.cloned.1.call-start = ((), (), s32[]{:S(2)}) async-start(), calls=%async_computation.5 | async-start | bytes 5529600 | tf_op jit(solution)/shard_map/all_gather | solution.py:67
Sparse Core Ops, SparseCore 0:
  10.3 180.2 all-gather.2
  205.2 47.0 reduce-scatter.1
  259.5 49.7 all-gather.4
where the time goes:
time: 353 us
  waiting for transfers between devices  180 us (51%)
  blocking collectives  113 us (32%)
  matrix products  30.3 us (9%)
  between operations  13.8 us (4%)
  other arithmetic  10.8 us (3%)
  local copies, waits for them, and re-layouts  5.15 us (1%)
    all_gather x1, waiting for transfers between devices, per_device(): whole_cotangent = lax.all_gather(grad_out, 'row', axis=0, tiled=True)  132 us
    all_to_all x1, blocking collectives, sum_at_owner(): lax.all_to_all(parts, axis, split_axis=0, concat_axis=0, tiled=True)  62.6 us
    all_to_all x1, blocking collectives, from_everyone(): lax.all_to_all(jnp.broadcast_to(array[None], (count, *array.shape)), axis...  50.5 us
    reduce_scatter x1, waiting for transfers between devices, per_device(): lax.psum_scatter(lax.dot_general(picked, whole_cotangent, (((0,), (0,)),...  47.2 us
    dot_general x1, matrix products, per_device(): lax.dot_general(picked, weight, (((1,), (1,)), ((), ())), preferred_eleme...  15.9 us
    dot_general x1, matrix products, per_device(): lax.dot_general(picked, whole_cotangent, (((0,), (0,)), ((), ())), prefer...  14.4 us
  transfers between devices with their start and end apart: 3, of which 2 were waited for; matrix products, arithmetic and copies ran while one was open for 6% of the time, Pallas kernels for 0%

commit v1 on v0

--- a/solution.py
+++ b/solution.py
@@ -38,7 +38,8 @@
 def per_device(acts, grad_out, weight, master, moment_one, moment_two):
     whole_acts = gathered_copies(acts, "col", 0)
     tokens_total = acts.shape[0] * lax.axis_size("col") * lax.axis_size("depth")
-    whole_cotangent = lax.all_gather(grad_out, "row", axis=0, tiled=True)
+    sent = jnp.stack([grad_out] * lax.axis_size("row"))
+    whole_cotangent = jnp.concatenate(lax.all_to_all(sent, "row", 0, 0), axis=0)
     picked = whole_cotangent
     input_sum = sum_at_owner(
         lax.dot_general(

time: 353 us -> 375 us (1.062)
  blocking collectives: 113 us -> 260 us
  waiting for transfers between devices: 180 us -> 49.9 us
  local copies, waits for them, and re-layouts: 5.15 us -> 12.3 us
    all_to_all x0 -> x1, blocking collectives: none -> 163 us  [per_device(): whole_cotangent = jnp.concatenate(lax.all_to_all(sent, 'row', 0, 0), axis=0)]
    all_gather x1 -> x0, waiting for transfers between devices: 132 us -> none  [per_device(): whole_cotangent = lax.all_gather(grad_out, 'row', axis=0, tiled=True)]
    all_to_all x1, blocking collectives: 50.5 us -> 34.9 us  [from_everyone(): lax.all_to_all(jnp.broadcast_to(array[None], (count, *array.shape)), axis...]
    unnamed x5 -> x7, local copies, waits for them, and re-layouts: 4.95 us -> 9.72 us
  transfers between devices with their start and end apart: 3 -> 2, of which waited for: 2 -> 1; matrix products, arithmetic and copies ran while one was open for 6% -> 5% of each run, Pallas kernels for 0% -> 0%
where the time goes in v1:
time: 375 us
  blocking collectives  260 us (69%)
  waiting for transfers between devices  49.9 us (13%)
  matrix products  27.5 us (7%)
  between operations  14.1 us (4%)
  local copies, waits for them, and re-layouts  12.3 us (3%)
  other arithmetic  10.8 us (3%)
    all_to_all x1, blocking collectives, per_device(): whole_cotangent = jnp.concatenate(lax.all_to_all(sent, 'row', 0, 0), axis=0)  163 us
    all_to_all x1, blocking collectives, sum_at_owner(): lax.all_to_all(parts, axis, split_axis=0, concat_axis=0, tiled=True)  62.6 us
    reduce_scatter x1, waiting for transfers between devices, per_device(): lax.psum_scatter(lax.dot_general(picked, whole_cotangent, (((0,), (0,)),...  49.9 us
    all_to_all x1, blocking collectives, from_everyone(): lax.all_to_all(jnp.broadcast_to(array[None], (count, *array.shape)), axis...  34.9 us
    dot_general x1, matrix products, per_device(): lax.dot_general(picked, weight, (((1,), (1,)), ((), ())), preferred_eleme...  15.9 us
    dot_general x1, matrix products, per_device(): lax.dot_general(picked, whole_cotangent, (((0,), (0,)), ((), ())), prefer...  11.5 us
    unnamed x7, local copies, waits for them, and re-layouts  9.72 us
  transfers between devices with their start and end apart: 2, of which 1 were waited for; matrix products, arithmetic and copies ran while one was open for 5% of the time, Pallas kernels for 0%

profile of v1, /device:TPU:1, one launch (start us, length us, event | category | flops | bytes accessed | tf_op | source)
XLA Modules:
  0.0 374.7 jit_solution(14685978226077649701)
XLA Ops:
  7.2 0.0 reduce-scatter.2.cloned.1.call-start
  7.2 1.3 broadcast_in_dim.2
  8.5 0.0 copy-start.2
  8.5 34.9 %all_to_all.15 = bf16[4,512,640]{2,1,0:T(8,128)(2,1)S(1)} all-to-all(bf16[4,512,640]{2,1,0:T(8,128)(2,1)S(1)} %broadcast_in_dim.2), channel_id=1, replica_groups=mesh['row'=8,'col'=4,'depth'=4] {'col'}, dimensions={0} | all-to-all | bytes 5242880 | tf_op jit(solution)/shard_map/all_to_all | solution.py:18
  43.4 0.0 copy-done.2
  43.4 1.3 stack.2
  44.7 162.6 %all_to_all.16 = bf16[8,256,3456]{2,1,0:T(8,128)(2,1)S(1)} all-to-all(bf16[8,256,3456]{2,1,0:T(8,128)(2,1)S(1)} %stack.2), channel_id=1, replica_groups=mesh['row'=8,'col'=4,'depth'=4] {'row'}, dimensions={0} | all-to-all | bytes 28311552 | tf_op jit(solution)/shard_map/all_to_all | solution.py:42
  207.3 0.0 copy-start
  207.3 5.1 %copy-done = bf16[8,256,3456]{2,1,0:T(8,128)(2,1)} copy-done((bf16[8,256,3456]{2,1,0:T(8,128)(2,1)}, bf16[8,256,3456]{2,1,0:T(8,128)(2,1)S(1)}, u32[]{:S(2)}) %copy-start) | copy-done | bytes 14155800
  212.4 11.5 %convolution_convert_fusion = bf16[640,3456]{1,0:T(8,128)(2,1)} fusion(bf16[2048,640]{1,0:T(8,128)(2,1)S(1)} %bitcast.11, bf16[2048,3456]{1,0:T(8,128)(2,1)S(1)} %bitcast.9), kind=kOutput, calls=%fused_computation | convolution fusion | flops 9061908480 | bytes 21200896 | tf_op jit(solution)/shard_map/dot_general | solution.py:53
  223.9 0.0 copy-start.1
  223.9 0.0 reduce-scatter.2.cloned.1.call-update
  223.9 0.0 all-gather.2.cloned.1.call-start
  224.0 49.9 %reduce-scatter.2.cloned.1.call-done = bf16[160,3456]{1,0:T(8,128)(2,1)} async-done(((bf16[640,3456]{1,0:T(8,128)(2,1)}), bf16[160,3456]{1,0:T(8,128)(2,1)}) %reduce-scatter.2.cloned.1.call-update) | async-done | bytes 1105936 | tf_op jit(solution)/shard_map/reduce_scatter | solution.py:52
  273.8 0.0 copy-done.1
  273.8 7.0 %fusion.5 = (bf16[160,3456]{1,0:T(8,128)(2,1)}, f32[160,3456]{1,0:T(8,128)}, f32[160,3456]{1,0:T(8,128)}, f32[160,3456]{1,0:T(8,128)}) fusion(f32[160,3456]{1,0:T(8,128)S(1)} %copy-done.1, bf16[160,3456]{1,0:T(8,128)(2,1)} %reduce-scatter.2.cloned.1.call-done, f32[160,3456]{1,0:T(8,128)} %param.10, f32[160,3456]{1,0:T(8,128)} %param.11), kind=kLoop, calls=%fused_computation.10 | loop fusion | flops 9953280 | bytes 15482880 | tf_op jit(solution)/shard_map/convert_element_type | solution.py:68
  280.9 0.0 all-gather.2.cloned.1.call-update
  280.9 15.9 %fusion = f32[4,512,640]{2,1,0:T(8,128)S(1)} fusion(bf16[4,512,3456]{2,1,0:T(8,128)(2,1)} %bitcast.10, bf16[640,3456]{1,0:T(8,128)(2,1)} %param.8), kind=kOutput, calls=%fused_computation.1 | convolution fusion | flops 9059696640 | bytes 23822336 | tf_op jit(solution)/shard_map/dot_general | solution.py:45
  296.8 62.6 %all_to_all.17 = f32[4,512,640]{2,1,0:T(8,128)} all-to-all(f32[4,512,640]{2,1,0:T(8,128)S(1)} %fusion), channel_id=1, replica_groups=mesh['row'=8,'col'=4,'depth'=4] {'col'}, dimensions={0} | all-to-all | bytes 10485760 | tf_op jit(solution)/shard_map/all_to_all | solution.py:34
  359.4 3.8 %reduce_sum.9 = bf16[512,640]{1,0:T(8,128)(2,1)} reduce(f32[4,512,640]{2,1,0:T(8,128)} %all_to_all.17, f32[]{:T(128)} %constant.4.clone.1), dimensions={0}, to_apply=%region_0.0 | reduce | flops 983040 | bytes 5898244 | tf_op jit(solution)/shard_map/reduce_sum | solution.py:35
  363.2 0.0 all-gather.2.cloned.1.call-done
  363.2 4.6 %copy.12 = bf16[640,3456]{1,0:T(8,128)(2,1)} copy(bf16[640,3456]{1,0:T(8,128)(2,1)} %all-gather.2.cloned.1.call-done) | data formatting | bytes 8847360
Async XLA Ops:
  7.2 266.7 %reduce-scatter.2.cloned.1.call-start = ((), (), s32[]{:S(2)}) async-start(), calls=%async_computation.4 | async-start | bytes 5529600 | tf_op jit(solution)/shard_map/reduce_scatter | solution.py:52
  8.5 34.9 %copy-start.2 = (bf16[256,3456]{1,0:T(8,128)(2,1)S(1)}, bf16[256,3456]{1,0:T(8,128)(2,1)}, u32[]{:S(2)}) copy-start(bf16[256,3456]{1,0:T(8,128)(2,1)} %param.7) | copy-start | bytes 5308420
  207.3 5.1 %copy-start = (bf16[8,256,3456]{2,1,0:T(8,128)(2,1)}, bf16[8,256,3456]{2,1,0:T(8,128)(2,1)S(1)}, u32[]{:S(2)}) copy-start(bf16[8,256,3456]{2,1,0:T(8,128)(2,1)S(1)} %all_to_all.16) | copy-start | bytes 42467332
  223.9 50.0 %copy-start.1 = (f32[160,3456]{1,0:T(8,128)S(1)}, f32[160,3456]{1,0:T(8,128)}, u32[]{:S(2)}) copy-start(f32[160,3456]{1,0:T(8,128)} %param.9) | copy-start | bytes 6635524
  223.9 139.3 %all-gather.2.cloned.1.call-start = ((), (), s32[]{:S(2)}) async-start(), calls=%async_computation.5 | async-start | bytes 5529600 | tf_op jit(solution)/shard_map/all_gather | solution.py:68
Sparse Core Ops, SparseCore 0:
  224.0 49.7 reduce-scatter.1
  281.0 49.7 all-gather.1
